TPU v7x, 32 devices: a whole 2x2x4 slice. The times are simulated.
32 devices in a mesh: ep: 16 (over z, y, x), dp: 2 (over core).
Axes of the slice: x: 2, y: 2, z: 4, core: 2. Of those that a mesh axis runs over, the one named last changes fastest.
Arguments:
- layer_input: bfloat16 [2048, 3584], P('ep'), may hold values from -6 to 6
- out_grad: bfloat16 [2048, 3584], P('ep'), may hold values from -6 to 6
- expert_ids: int32 [2048, 8], P('ep'), may hold values from 0 to 15, all different within a row; in each aligned block of 128 rows (0 to 127, 128 to 255, ...) at most 80 rows name the same one
- gate_probs: float32 [2048, 8], P('ep'), may hold values from 0.1 to 1
- gate_proj: bfloat16 [16, 3584, 1024], P('ep'), may hold values from -0.09375 to 0.09375
- up_proj: bfloat16 [16, 3584, 1024], P('ep'), may hold values from -0.09375 to 0.09375
- down_proj: bfloat16 [16, 1024, 3584], P('ep'), may hold values from -0.1875 to 0.1875
Outputs:
- input_grad: bfloat16 [2048, 3584], P('ep', 'dp')
Inputs may be any that keep to these rules, and one draw needn't show every extreme that they name: `expert_ids`: each row names 8 different experts. The 128 rows of one device name one expert at most 80 times, and in every draw some device's rows name some expert exactly 80 times.
All inputs are finite; a program needn't handle non-finite values.
Results may differ from a plain program's by a relative error of at most 0.0058.
Values may be sent and summed in bfloat16 or wider, within the bound.
A program may use at most 192 MiB of HBM per device.

v0:
```python
import jax
import jax.numpy as jnp
from jax import lax
from jax.sharding import PartitionSpec as P


def slot_ranks(flat_ids, experts_count):
    onehot = (flat_ids[:, None] == jnp.arange(experts_count, dtype=jnp.int32)[None, :]).astype(
        jnp.int32
    )
    running = jnp.cumsum(onehot, axis=0)
    return jnp.sum((running - 1) * onehot, axis=1)


def expert_backward(in_rows, grad_rows, gate_mat, up_mat, down_mat):
    gate_pre = jnp.dot(in_rows, gate_mat, preferred_element_type=jnp.float32)
    up_pre = jnp.dot(in_rows, up_mat, preferred_element_type=jnp.float32)
    hidden_grad = lax.dot_general(
        grad_rows, down_mat, (((1,), (1,)), ((), ())), preferred_element_type=jnp.float32
    )
    sigmoid = jax.nn.sigmoid(gate_pre)
    gate_grad = (hidden_grad * up_pre * sigmoid * (1.0 + gate_pre * (1.0 - sigmoid))).astype(
        jnp.bfloat16
    )
    up_grad = (hidden_grad * gate_pre * sigmoid).astype(jnp.bfloat16)
    back_gate = lax.dot_general(
        gate_grad, gate_mat, (((1,), (1,)), ((), ())), preferred_element_type=jnp.float32
    )
    back_up = lax.dot_general(
        up_grad, up_mat, (((1,), (1,)), ((), ())), preferred_element_type=jnp.float32
    )
    return back_gate + back_up


def body(layer_input, out_grad, expert_ids, gate_probs, gate_proj, up_proj, down_proj):
    experts_count = lax.axis_size("ep")
    tok_rows, features = layer_input.shape
    top_count = expert_ids.shape[1]
    capacity = 2 * ((5 * tok_rows * top_count + 8 * experts_count - 1) // (8 * experts_count))
    flat_ids = expert_ids.reshape(-1)
    route_count = flat_ids.shape[0]
    slot_rank = slot_ranks(flat_ids, experts_count)
    core_index = lax.axis_index("dp")
    span = capacity // 2
    local_rank = slot_rank - core_index * span
    inside = (local_rank >= 0) & (local_rank < span)
    slot_index = flat_ids * span + jnp.clip(local_rank, 0, span - 1)
    gate_mat, up_mat, down_mat = (gate_proj[0], up_proj[0], down_proj[0])
    route_weight = jnp.where(inside, gate_probs.reshape(-1), 0.0)
    target = jnp.where(inside, slot_index, experts_count * span)
    route_token = jnp.arange(route_count, dtype=jnp.int32) // top_count
    slot_token = (
        jnp.full((experts_count * span,), tok_rows, jnp.int32)
        .at[target]
        .set(route_token, mode="drop")
    )
    padded_in = jnp.concatenate([layer_input, jnp.zeros((1, features), layer_input.dtype)], 0)
    padded_grad = jnp.concatenate([out_grad, jnp.zeros((1, features), out_grad.dtype)], 0)
    in_buffer = jnp.take(padded_in, slot_token, axis=0).reshape(experts_count, span, features)
    grad_buffer = jnp.take(padded_grad, slot_token, axis=0).reshape(experts_count, span, features)
    in_rows = lax.all_to_all(in_buffer, "ep", split_axis=0, concat_axis=0, tiled=True)
    grad_rows = lax.all_to_all(grad_buffer, "ep", split_axis=0, concat_axis=0, tiled=True)
    sources = in_rows.shape[0]
    items = in_rows.shape[1]
    partial_value = expert_backward(
        in_rows.reshape(-1, features), grad_rows.reshape(-1, features), gate_mat, up_mat, down_mat
    )
    partial_value = partial_value.reshape(sources, items, features)
    returned = lax.all_to_all(
        partial_value.astype(jnp.bfloat16), "ep", split_axis=0, concat_axis=0, tiled=True
    )
    slot_rows = returned.reshape(experts_count * span, returned.shape[2])
    picked = jnp.take(slot_rows, slot_index, axis=0).astype(jnp.float32) * route_weight[:, None]
    summed = picked.reshape(tok_rows, top_count, slot_rows.shape[1]).sum(axis=1)
    summed = lax.psum_scatter(summed, "dp", scatter_dimension=1, tiled=True)
    return summed.astype(jnp.bfloat16)


def solution(mesh):
    placed = (
        P("ep", None),
        P("ep", None),
        P("ep", None),
        P("ep", None),
        P("ep", None, None),
        P("ep", None, None),
        P("ep", None, None),
    )
    return jax.shard_map(body, mesh=mesh, in_specs=placed, out_specs=P("ep", "dp"), check_vma=False)
```

profile of v0, /device:TPU:11, one launch (start us, length us, event | category | flops | bytes accessed | tf_op | source)
XLA Modules:
  0.0 451.4 jit_solution(9607886619872433837)
XLA Ops:
  6.5 0.8 copy.18
  7.3 0.1 eq.26
  7.4 0.1 reshape.154
  7.5 4.5 %reduce-window.6 = s32[16,8,128]{2,1,0:T(8,128)S(1)} reduce-window(s32[16,8,128]{2,1,0:T(8,128)S(1)} %fusion.20, s32[]{:T(128)} %constant.35.clone.1), window={size=1x1x128 pad=0_0x0_0x127_0}, to_apply=%region_0.0 | reduce-window | flops 2080768 | bytes 131076 | tf_op jit(solution)/shard_map/reduce-window
  12.0 0.1 slice.14
  12.1 0.1 copy.20
  12.3 0.1 copy.21
  12.4 0.1 add_add_fusion
  12.5 0.7 broadcast_multiply_fusion
  13.2 0.1 copy.24
  13.3 0.1 mul.56
  13.4 4.3 scatter_custom_fusion
  17.8 1.2 concatenate.7
  19.0 1.2 concatenate.6
  20.3 5.1 %gather_fusion.2 = bf16[640,3584]{1,0:T(8,128)(2,1)} fusion(bf16[129,3584]{1,0:T(8,128)(2,1)S(1)} %concatenate.7, s32[1024]{0:T(1024)S(1)} %pad_clamp_fusion), kind=kCustom, calls=%fused_computation.1.clone | custom fusion | bytes 9177600 | tf_op jit(solution)/shard_map/jit(_take)/gather | solution.py:59
  25.4 5.1 %gather_fusion.1 = bf16[640,3584]{1,0:T(8,128)(2,1)} fusion(bf16[129,3584]{1,0:T(8,128)(2,1)S(1)} %concatenate.6, s32[1024]{0:T(1024)S(1)} %pad_clamp_fusion), kind=kCustom, calls=%fused_computation.clone | custom fusion | bytes 9177600 | tf_op jit(solution)/shard_map/jit(_take)/gather | solution.py:60
  30.5 6.7 %broadcast_select_fusion.1 = (bf16[640,3584]{1,0:T(8,128)(2,1)}, bf16[640,3584]{1,0:T(8,128)(2,1)S(1)}) fusion(bf16[640,3584]{1,0:T(8,128)(2,1)} %gather_fusion.1, pred[640]{0:T(1024)(128)(4,1)S(1)} %compare_and_fusion, bf16[640,3584]{1,0:T(8,128)(2,1)} %gather_fusion.2), kind=kLoop, calls=%fused_computation.18 | loop fusion | flops 4587520 | bytes 18350720 | tf_op jit(solution)/shard_map/jit(_take)/select_n | solution.py:60
  37.3 106.5 %all_to_all.15 = bf16[16,40,3584]{2,1,0:T(8,128)(2,1)} all-to-all(bf16[16,40,3584]{2,1,0:T(8,128)(2,1)S(1)} %bitcast.50), channel_id=1, replica_groups=mesh['ep'=16,'dp'=2] {'ep'}, dimensions={0} | all-to-all | bytes 9175040 | tf_op jit(solution)/shard_map/all_to_all | solution.py:61
  143.8 5.4 %all-to-all-start = ((bf16[16,40,3584]{2,1,0:T(8,128)(2,1)}), bf16[16,40,3584]{2,1,0:T(8,128)(2,1)}, u32[]{:S(2)}, u32[]{:S(2)}) async-start(bf16[16,40,3584]{2,1,0:T(8,128)(2,1)} %bitcast.49), calls=%async_computation | async-start | bytes 9175040 | tf_op jit(solution)/shard_map/all_to_all | solution.py:62
  149.2 10.8 %fusion.2 = f32[640,1024]{1,0:T(8,128)} fusion(bf16[640,3584]{1,0:T(8,128)(2,1)} %bitcast.52, bf16[1,3584,1024]{2,1,0:T(8,128)(2,1)} %param.13), kind=kOutput, calls=%fused_computation.9 | convolution fusion | flops 4697620480 | bytes 14548992 | tf_op jit(solution)/shard_map/dot_general | solution.py:16
  160.0 85.5 %all-to-all-done = bf16[16,40,3584]{2,1,0:T(8,128)(2,1)} async-done(((bf16[16,40,3584]{2,1,0:T(8,128)(2,1)}), bf16[16,40,3584]{2,1,0:T(8,128)(2,1)}, u32[]{:S(2)}, u32[]{:S(2)}) %all-to-all-start) | async-done | bytes 4587552 | tf_op jit(solution)/shard_map/all_to_all | solution.py:62
  245.5 10.9 %fusion.8 = f32[640,1024]{1,0:T(8,128)} fusion(bf16[640,3584]{1,0:T(8,128)(2,1)} %bitcast.5, bf16[1,1024,3584]{2,1,0:T(8,128)(2,1)} %param.15), kind=kOutput, calls=%fused_computation.15 | convolution fusion | flops 4697620480 | bytes 14548992 | tf_op jit(solution)/shard_map/dot_general | solution.py:18
  256.5 19.4 %fusion = f32[640,3584]{1,0:T(8,128)} fusion(bf16[1,3584,1024]{2,1,0:T(8,128)(2,1)} %param.13, f32[640,1024]{1,0:T(8,128)} %fusion.2, f32[640,1024]{1,0:T(8,128)} %fusion.8, bf16[640,3584]{1,0:T(8,128)(2,1)} %bitcast.53, bf16[1,3584,1024]{2,1,0:T(8,128)(2,1)} %param.14), kind=kOutput, calls=%fused_computation.7 | convolution fusion | flops 9401794560 | bytes 33685504 | tf_op jit(solution)/shard_map/dot_general | solution.py:26
  275.9 14.4 %add_convert_fusion = bf16[640,3584]{1,0:T(8,128)(2,1)} fusion(f32[640,3584]{1,0:T(8,128)} %fusion, bf16[1,3584,1024]{2,1,0:T(8,128)(2,1)} %param.14, f32[640,1024]{1,0:T(8,128)} %fusion.8, f32[640,1024]{1,0:T(8,128)} %fusion.2), kind=kOutput, calls=%fused_computation.5 | convolution fusion | flops 4706140160 | bytes 26345472 | tf_op jit(solution)/shard_map/dot_general | solution.py:29
  290.3 0.0 copy-start.1
  290.3 0.0 copy-start
  290.3 9.9 %all-to-all-start.2 = ((bf16[16,40,3584]{2,1,0:T(8,128)(2,1)}), bf16[16,40,3584]{2,1,0:T(8,128)(2,1)}, u32[]{:S(2)}, u32[]{:S(2)}) async-start(bf16[16,40,3584]{2,1,0:T(8,128)(2,1)} %bitcast.51), calls=%async_computation.2 | async-start | bytes 9175040 | tf_op jit(solution)/shard_map/all_to_all | solution.py:69
  300.2 0.0 reduce-scatter.2.cloned.1.call-start
  300.3 0.1 and.41
  300.4 0.1 min.14
  300.4 0.0 copy-done.1
  300.5 0.1 copy.25
  300.6 0.0 copy-done
  300.6 0.1 copy.23
  300.8 97.4 %all-to-all-done.2 = bf16[16,40,3584]{2,1,0:T(8,128)(2,1)} async-done(((bf16[16,40,3584]{2,1,0:T(8,128)(2,1)}), bf16[16,40,3584]{2,1,0:T(8,128)(2,1)}, u32[]{:S(2)}, u32[]{:S(2)}) %all-to-all-start.2) | async-done | bytes 4587552 | tf_op jit(solution)/shard_map/all_to_all | solution.py:69
  398.2 16.7 %gather_fusion = bf16[1024,3584]{1,0:T(8,128)(2,1)} fusion(bf16[640,3584]{1,0:T(8,128)(2,1)} %bitcast.12, s32[1024]{0:T(1024)S(1)} %broadcast_clamp_fusion), kind=kCustom, calls=%fused_computation.2 | custom fusion | bytes 14684160 | tf_op jit(solution)/shard_map/jit(_take)/gather | solution.py:73
  414.9 13.6 %multiply_reduce_fusion = f32[128,3584]{1,0:T(8,128)} fusion(bf16[1024,3584]{1,0:T(8,128)(2,1)} %gather_fusion, f32[128,8]{1,0:T(8,128)S(1)} %broadcast_select_fusion.2, pred[128,8]{1,0:T(8,128)(4,1)S(1)} %copy.23), kind=kLoop, calls=%fused_computation.4 | loop fusion | flops 14221312 | bytes 9180160 | tf_op jit(solution)/shard_map/reduce_sum | solution.py:74
  428.5 0.0 reduce-scatter.2.cloned.1.call-update
  428.5 14.1 %reduce-scatter.2.cloned.1.call-done = f32[128,1792]{1,0:T(8,128)} async-done(((f32[128,3584]{1,0:T(8,128)}), f32[128,1792]{1,0:T(8,128)}) %reduce-scatter.2.cloned.1.call-update) | async-done | bytes 917520 | tf_op jit(solution)/shard_map/reduce_scatter | solution.py:75
  442.6 2.0 convert_element_type.30
  (15 shorter events, 0.2 us)
Async XLA Ops:
  143.8 101.7 %all-to-all-start = ((bf16[16,40,3584]{2,1,0:T(8,128)(2,1)}), bf16[16,40,3584]{2,1,0:T(8,128)(2,1)}, u32[]{:S(2)}, u32[]{:S(2)}) async-start(bf16[16,40,3584]{2,1,0:T(8,128)(2,1)} %bitcast.49), calls=%async_computation | async-start | bytes 9175040 | tf_op jit(solution)/shard_map/all_to_all | solution.py:62
  290.3 10.2 %copy-start.1 = (f32[128,8]{0,1:T(8,128)S(1)}, f32[128,8]{0,1:T(8,128)}, u32[]{:S(2)}) copy-start(f32[128,8]{0,1:T(8,128)} %param.12) | copy-start | bytes 12292
  290.3 10.3 %copy-start = (s32[128,8]{0,1:T(8,128)S(1)}, s32[128,8]{0,1:T(8,128)}, u32[]{:S(2)}) copy-start(s32[128,8]{0,1:T(8,128)} %param.11) | copy-start | bytes 12292
  290.3 107.9 %all-to-all-start.2 = ((bf16[16,40,3584]{2,1,0:T(8,128)(2,1)}), bf16[16,40,3584]{2,1,0:T(8,128)(2,1)}, u32[]{:S(2)}, u32[]{:S(2)}) async-start(bf16[16,40,3584]{2,1,0:T(8,128)(2,1)} %bitcast.51), calls=%async_computation.2 | async-start | bytes 9175040 | tf_op jit(solution)/shard_map/all_to_all | solution.py:69
  300.2 142.4 %reduce-scatter.2.cloned.1.call-start = ((), (), s32[]{:S(2)}) async-start(), calls=%async_computation.4 | async-start | bytes 2752512 | tf_op jit(solution)/shard_map/reduce_scatter | solution.py:75
Sparse Core Ops, SparseCore 0:
  428.6 13.9 reduce-scatter.1
where the time goes:
time: 453 us; the launch traced here: 451 us
  waiting for transfers between devices  197 us (43%)
  blocking collectives  107 us (24%)
  matrix products  55.6 us (12%)
  local copies, waits for them, and re-layouts  35.6 us (8%)
  other arithmetic  27.8 us (6%)
  starting transfers between devices  15.4 us (3%)
  between operations  13.5 us (3%)
    all_to_all x1, blocking collectives, body(): lax.all_to_all(in_buffer, 'ep', split_axis=0, concat_axis=0, tiled=True)  107 us
    all_to_all x1, waiting for transfers between devices, body(): lax.all_to_all(partial_value.astype(jnp.bfloat16), 'ep', split_axis=0, co...  97.4 us
    all_to_all x1, waiting for transfers between devices, body(): lax.all_to_all(grad_buffer, 'ep', split_axis=0, concat_axis=0, tiled=True)  85.5 us
    dot_general x1, matrix products, expert_backward(): lax.dot_general(gate_grad, gate_mat, (((1,), (1,)), ((), ())), preferred_...  19.4 us
    gather x1, local copies, waits for them, and re-layouts, body(): jnp.take(slot_rows, slot_index, axis=0).astype(jnp.float32)  16.7 us
    dot_general x1, matrix products, expert_backward(): lax.dot_general(up_grad, up_mat, (((1,), (1,)), ((), ())), preferred_elem...  14.4 us
    reduce_scatter x1, waiting for transfers between devices, body(): summed = lax.psum_scatter(summed, 'dp', scatter_dimension=1, tiled=True)  14.1 us
    reduce_sum x1, other arithmetic, body(): summed = picked.reshape(tok_rows, top_count, slot_rows.shape[1]).sum(axis=1)  13.6 us
  transfers between devices with their start and end apart: 3, of which 3 were waited for; matrix products, arithmetic and copies ran while one was open for 3% of the time, Pallas kernels for 0%

commit v1 on v0

v1 whole, which is shorter than its diff:
```python
import jax
import jax.numpy as jnp
from jax import lax
from jax.sharding import PartitionSpec as P


def body(layer_input, out_grad, expert_ids, gate_probs, gate_proj, up_proj, down_proj):
    experts = lax.axis_size("ep")
    halves = lax.axis_size("dp")
    tok_rows, features = layer_input.shape
    half = tok_rows // halves
    core = lax.axis_index("dp")
    start = core * half
    mine_in = lax.dynamic_slice_in_dim(layer_input, start, half, 0)
    mine_grad = lax.dynamic_slice_in_dim(out_grad, start, half, 0)
    ids = lax.dynamic_slice_in_dim(expert_ids, start, half, 0)
    probs = lax.dynamic_slice_in_dim(gate_probs, start, half, 0)
    names = jnp.arange(experts, dtype=jnp.int32)
    table = jnp.sum(
        jnp.where(ids[None, :, :] == names[:, None, None], probs[None, :, :], 0.0), axis=2
    )
    weight = lax.all_to_all(table, "ep", split_axis=0, concat_axis=0, tiled=True).reshape(-1)
    in_rows = lax.all_gather(mine_in, "ep", axis=0, tiled=True)
    grad_rows = lax.all_gather(mine_grad, "ep", axis=0, tiled=True)
    gate_mat, up_mat, down_mat = (gate_proj[0], up_proj[0], down_proj[0])
    nt = (((1,), (1,)), ((), ()))
    gate_pre = jnp.dot(in_rows, gate_mat, preferred_element_type=jnp.float32)
    up_pre = jnp.dot(in_rows, up_mat, preferred_element_type=jnp.float32)
    hidden_grad = lax.dot_general(grad_rows, down_mat, nt, preferred_element_type=jnp.float32)
    s = jax.nn.sigmoid(gate_pre)
    gate_grad = (hidden_grad * up_pre * s * (1.0 + gate_pre * (1.0 - s))).astype(jnp.bfloat16)
    up_grad = (hidden_grad * gate_pre * s).astype(jnp.bfloat16)
    back = lax.dot_general(gate_grad, gate_mat, nt, preferred_element_type=jnp.float32)
    back = back + lax.dot_general(up_grad, up_mat, nt, preferred_element_type=jnp.float32)
    back = (back * weight[:, None]).astype(jnp.bfloat16)
    mine = lax.psum_scatter(back, "ep", scatter_dimension=0, tiled=True)
    return lax.all_to_all(mine, "dp", split_axis=1, concat_axis=0, tiled=True)


def solution(mesh):
    row = P("ep", None)
    mat = P("ep", None, None)
    return jax.shard_map(
        body, mesh=mesh, in_specs=(row, row, row, row, mat, mat, mat), out_specs=P("ep", "dp"), check_vma=False
    )
```

time: 453 us -> 443 us (0.978)
  waiting for transfers between devices: 197 us -> 338 us
  blocking collectives: 107 us -> 15.3 us
  local copies, waits for them, and re-layouts: 35.6 us -> 7.81 us
  other arithmetic: 27.8 us -> 0.72 us
  starting transfers between devices: 15.4 us -> 0.09 us
  matrix products: 55.6 us -> 67.4 us
    all_to_all x2 -> x0, waiting for transfers between devices: 183 us -> none  [the longest x1 97.4 us: body(): lax.all_to_all(partial_value.astype(jnp.bfloat16), 'ep', split_axis=0, co...]
    all_gather x0 -> x2, waiting for transfers between devices: none -> 178 us  [the longest x1 90.3 us: body(): in_rows = lax.all_gather(mine_in, 'ep', axis=0, tiled=True)]
    reduce_scatter x1, waiting for transfers between devices: 14.1 us -> 160 us  [body(): mine = lax.psum_scatter(back, 'ep', scatter_dimension=0, tiled=True)]
    all_to_all x1 -> x2, blocking collectives: 107 us -> 15.3 us  [the longest x1 10.6 us: body(): lax.all_to_all(table, 'ep', split_axis=0, concat_axis=0, tiled=True)]
    gather x3 -> x0, local copies, waits for them, and re-layouts: 26.9 us -> none  [the longest x1 16.7 us: body(): jnp.take(slot_rows, slot_index, axis=0).astype(jnp.float32)]
    all_to_all x2 -> x0, starting transfers between devices: 15.3 us -> none  [the longest x1 9.94 us: body(): lax.all_to_all(partial_value.astype(jnp.bfloat16), 'ep', split_axis=0, co...]
    reduce_sum x2 -> x1, other arithmetic: 13.6 us -> 0.03 us  [body(): jnp.sum(jnp.where(ids[None, :, :] == names[:, None, None], probs[None, :,...]
    dot_general x4 -> x5, matrix products: 55.6 us -> 67.4 us  [the longest x1 17.7 us: body(): lax.dot_general(up_grad, up_mat, nt, preferred_element_type=jnp.float32)]
  transfers between devices with their start and end apart: 3 -> 3, of which waited for: 3 -> 3; matrix products, arithmetic and copies ran while one was open for 3% -> 4% of each run, Pallas kernels for 0% -> 0%
where the time goes in v1:
time: 443 us; the launch traced here: 442 us
  waiting for transfers between devices  338 us (76%)
  matrix products  67.4 us (15%)
  blocking collectives  15.3 us (3%)
  between operations  13.2 us (3%)
  local copies, waits for them, and re-layouts  7.81 us (2%)
    reduce_scatter x1, waiting for transfers between devices, body(): mine = lax.psum_scatter(back, 'ep', scatter_dimension=0, tiled=True)  160 us
    all_gather x1, waiting for transfers between devices, body(): in_rows = lax.all_gather(mine_in, 'ep', axis=0, tiled=True)  90.3 us
    all_gather x1, waiting for transfers between devices, body(): grad_rows = lax.all_gather(mine_grad, 'ep', axis=0, tiled=True)  87.5 us
    dot_general x1, matrix products, body(): lax.dot_general(up_grad, up_mat, nt, preferred_element_type=jnp.float32)  17.7 us
    dot_general x1, matrix products, body(): gate_pre = jnp.dot(in_rows, gate_mat, preferred_element_type=jnp.float32)  13.6 us
    dot_general x1, matrix products, body(): lax.dot_general(grad_rows, down_mat, nt, preferred_element_type=jnp.float32)  13.6 us
    dot_general x1, matrix products, body(): up_pre = jnp.dot(in_rows, up_mat, preferred_element_type=jnp.float32)  11.8 us
    dot_general x1, matrix products, body(): lax.dot_general(gate_grad, gate_mat, nt, preferred_element_type=jnp.float32)  10.7 us
  transfers between devices with their start and end apart: 3, of which 3 were waited for; matrix products, arithmetic and copies ran while one was open for 4% of the time, Pallas kernels for 0%

profile of v1, /device:TPU:11, one launch (start us, length us, event | category | flops | bytes accessed | tf_op | source)
XLA Modules:
  0.0 442.3 jit_solution(1134362332234248369)
XLA Ops:
  6.5 0.0 copy-start
  6.5 0.0 all-gather.3.cloned.1.call-start
  6.5 1.2 copy-done
  7.7 0.8 constant_dynamic-slice_fusion.3
  8.5 0.0 all-gather.3.cloned.1.call-update
  8.6 0.0 all-gather.5.cloned.1.call-start
  8.6 1.8 constant_dynamic-slice_fusion.2
  10.4 0.0 all-gather.5.cloned.1.call-update
  10.5 0.0 reduce-scatter.2.cloned.1.call-start
  10.5 0.8 constant_dynamic-slice_fusion.1
  11.3 0.8 constant_dynamic-slice_fusion
  12.1 10.6 %all_to_all.28 = f32[16,1,64]{2,1,0:T(1,128)S(1)} all-to-all(f32[16,1,64]{2,1,0:T(1,128)S(1)} %bitcast.32), channel_id=1, replica_groups=mesh['ep'=16,'dp'=2] {'ep'}, dimensions={0} | all-to-all | bytes 8192 | tf_op jit(solution)/shard_map/all_to_all | solution.py:22
  22.7 0.6 broadcast.14
  23.2 0.7 reduce.3
  23.9 0.1 mul.38
  24.0 87.5 %all-gather.3.cloned.1.call-done = bf16[1024,3584]{1,0:T(8,128)(2,1)} async-done(((bf16[64,3584]{1,0:T(8,128)(2,1)}), bf16[1024,3584]{1,0:T(8,128)(2,1)}) %all-gather.3.cloned.1.call-update) | async-done | bytes 7340048 | tf_op jit(solution)/shard_map/all_gather | solution.py:24
  111.5 13.6 %fusion.7 = f32[1024,1024]{1,0:T(8,128)} fusion(bf16[1024,3584]{1,0:T(8,128)(2,1)} %all-gather.3.cloned.1.call-done, bf16[1,1024,3584]{2,1,0:T(8,128)(2,1)} %param.13), kind=kOutput, calls=%fused_computation.8 | convolution fusion | flops 7516192768 | bytes 18874368 | tf_op jit(solution)/shard_map/dot_general | solution.py:29
  125.1 90.3 %all-gather.5.cloned.1.call-done = bf16[1024,3584]{1,0:T(8,128)(2,1)} async-done(((bf16[64,3584]{1,0:T(8,128)(2,1)}), bf16[1024,3584]{1,0:T(8,128)(2,1)}) %all-gather.5.cloned.1.call-update) | async-done | bytes 7340048 | tf_op jit(solution)/shard_map/all_gather | solution.py:23
  215.4 0.0 copy-start.2
  215.4 0.0 copy-start.3
  215.4 0.0 slice-start
  215.4 13.6 %fusion.2 = f32[1024,1024]{1,0:T(8,128)} fusion(bf16[1024,3584]{1,0:T(8,128)(2,1)} %all-gather.5.cloned.1.call-done, bf16[1,3584,1024]{2,1,0:T(8,128)(2,1)} %param.11), kind=kOutput, calls=%fused_computation.3 | convolution fusion | flops 7516192768 | bytes 18874368 | tf_op jit(solution)/shard_map/dot_general | solution.py:27
  229.0 0.0 copy-done.2
  229.0 0.0 copy-done.3
  229.0 0.0 slice-start.1
  229.0 11.8 %multiply_convert_fusion.2 = bf16[1024,1024]{1,0:T(8,128)(2,1)S(1)} fusion(f32[1024,1024]{1,0:T(8,128)} %fusion.2, f32[1024,1024]{1,0:T(8,128)S(1)} %copy-done.3, bf16[1024,3584]{1,0:T(8,128)(2,1)S(1)} %copy-done.2, bf16[1,3584,1024]{2,1,0:T(8,128)(2,1)} %param.12), kind=kOutput, calls=%fused_computation.11 | convolution fusion | flops 7526678528 | bytes 25165824 | tf_op jit(solution)/shard_map/dot_general | solution.py:28
  240.9 0.0 slice-done
  240.9 0.0 slice-done.1
  240.9 10.7 %fusion = f32[1024,3584]{1,0:T(8,128)} fusion(bf16[1024,1024]{1,0:T(8,128)(2,1)S(1)} %multiply_convert_fusion.2, bf16[1,3584,1024]{2,1,0:T(8,128)(2,1)S(1)} %bitcast.34), kind=kOutput, calls=%fused_computation.1 | convolution fusion | flops 7516192768 | bytes 24117248 | tf_op jit(solution)/shard_map/dot_general | solution.py:33
  251.6 0.0 copy-start.1
  251.6 17.7 %multiply_convert_fusion = bf16[1024,3584]{1,0:T(8,128)(2,1)} fusion(f32[1024,3584]{1,0:T(8,128)} %fusion, bf16[1,3584,1024]{2,1,0:T(8,128)(2,1)} %param.12, f32[1024]{0:T(1024)S(1)} %mul.38, f32[1024,1024]{1,0:T(8,128)} %fusion.7, f32[1024,1024]{1,0:T(8,128)} %fusion.2), kind=kOutput, calls=%fused_computation | convolution fusion | flops 7533494272 | bytes 37752832 | tf_op jit(solution)/shard_map/dot_general | solution.py:34
  269.3 0.0 reduce-scatter.2.cloned.1.call-update
  269.4 159.9 %reduce-scatter.2.cloned.1.call-done = bf16[64,3584]{1,0:T(8,128)(2,1)} async-done(((bf16[1024,3584]{1,0:T(8,128)(2,1)}), bf16[64,3584]{1,0:T(8,128)(2,1)}) %reduce-scatter.2.cloned.1.call-update) | async-done | bytes 458768 | tf_op jit(solution)/shard_map/reduce_scatter | solution.py:36
  429.2 1.0 copy.18
  430.3 4.7 %all_to_all.29 = bf16[64,2,1792]{2,0,1:T(8,128)(2,1)S(1)} all-to-all(bf16[64,2,1792]{2,0,1:T(8,128)(2,1)S(1)} %bitcast.29), channel_id=1, replica_groups=mesh['ep'=16,'dp'=2] {'dp'}, dimensions={1} | all-to-all | bytes 917504 | tf_op jit(solution)/shard_map/all_to_all | solution.py:37
  435.0 0.8 copy.20
  435.7 0.0 copy-done.1
  (2 shorter events, 0.0 us)
Async XLA Ops:
  6.5 1.2 copy-start
  6.5 105.0 %all-gather.3.cloned.1.call-start = ((), (), s32[]{:S(2)}) async-start(), calls=%async_computation.3 | async-start | bytes 7798784 | tf_op jit(solution)/shard_map/all_gather | solution.py:24
  8.6 206.9 %all-gather.5.cloned.1.call-start = ((), (), s32[]{:S(2)}) async-start(), calls=%async_computation.4 | async-start | bytes 7798784 | tf_op jit(solution)/shard_map/all_gather | solution.py:23
  10.5 418.8 %reduce-scatter.2.cloned.1.call-start = ((), (), s32[]{:S(2)}) async-start(), calls=%async_computation.5 | async-start | bytes 7798784 | tf_op jit(solution)/shard_map/reduce_scatter | solution.py:36
  215.4 13.6 %copy-start.2 = (bf16[1024,3584]{1,0:T(8,128)(2,1)S(1)}, bf16[1024,3584]{1,0:T(8,128)(2,1)}, u32[]{:S(2)}) copy-start(bf16[1024,3584]{1,0:T(8,128)(2,1)} %all-gather.5.cloned.1.call-done) | copy-start | bytes 22020100
  215.4 13.6 %copy-start.3 = (f32[1024,1024]{1,0:T(8,128)S(1)}, f32[1024,1024]{1,0:T(8,128)}, u32[]{:S(2)}) copy-start(f32[1024,1024]{1,0:T(8,128)} %fusion.7) | copy-start | bytes 12582916
  215.4 25.5 %slice-start = ((s8[7340032]{0:T(1024)(128)(4,1)}), s8[4194304]{0:T(1024)(128)(4,1)S(1)}, s32[]{:S(2)}) async-start(s8[7340032]{0:T(1024)(128)(4,1)} %bitcast.33), calls=%async_computation.6 | async-start | bytes 8388608
  229.0 11.9 %slice-start.1 = ((s8[7340032]{0:T(1024)(128)(4,1)}), s8[3145728]{0:T(1024)(128)(4,1)S(1)}, s32[]{:S(2)}) async-start(s8[7340032]{0:T(1024)(128)(4,1)} %bitcast.33), calls=%async_computation.7 | async-start | bytes 6291456
  251.6 184.1 %copy-start.1 = (bf16[128,3584]{1,0:T(8,128)(2,1)S(1)}, bf16[128,3584]{1,0:T(8,128)(2,1)}, u32[]{:S(2)}) copy-start(bf16[128,3584]{1,0:T(8,128)(2,1)} %param.8) | copy-start | bytes 2752516
Sparse Core Ops, SparseCore 0:
  10.0 101.4 all-gather.2
  114.2 101.1 all-gather.4
  269.5 159.7 reduce-scatter.1

commit v2 on v1

--- a/solution.py
+++ b/solution.py
@@ -1,10 +1,245 @@
+import functools
+
 import jax
 import jax.numpy as jnp
 from jax import lax
+from jax.experimental import pallas as pl
+from jax.experimental.pallas import tpu as pltpu
 from jax.sharding import PartitionSpec as P
 
-
-def body(layer_input, out_grad, expert_ids, gate_probs, gate_proj, up_proj, down_proj):
+MESH = pl.DeviceIdType.MESH
+NT = (((1,), (1,)), ((), ()))
+
+
+def flipped(z, j, planes):
+    result, bit = z, 1
+    while bit < planes:
+        if j & bit:
+            result = result + bit * (1 - 2 * ((z // bit) % 2))
+        bit *= 2
+    return result
+
+
+def kernel(planes, x_hbm, g_hbm, w_ref, wg_hbm, wu_hbm, wd_hbm, out_ref,
+           data, part, wgv, wuv, wdv, gg, ug, r1a, r1b, r2x, r2y, r3, fin,
+           send_sem, recv_sem, load_sem):
+    me, core = lax.axis_index("ep"), lax.axis_index("dp")
+    z, y, x = me // 4, (me // 2) % 2, me % 2
+    half, features = r2x.shape[1], r2x.shape[2]
+    hidden = wgv.shape[1]
+    cut = features // 2
+    peer_x, peer_y = z * 4 + y * 2 + (1 - x), z * 4 + (1 - y) * 2 + x
+    zs = [flipped(z, j, planes) for j in range(planes)]
+    peer_z = [zs[j] * 4 + y * 2 + x for j in range(planes)]
+
+    def block(j, dy, dx):
+        by = (1 - y) if dy else y
+        bx = (1 - x) if dx else x
+        return pl.ds(pl.multiple_of((zs[j] * 4 + by * 2 + bx) * half, half), half)
+
+    kinds = ("agz", "agx", "agy", "fa", "fb", "r1a", "r1b", "r2x", "r2y", "r3")
+    sent = []
+
+    def number(kind, j):
+        return len(kinds) * planes if kind == "dp" else kinds.index(kind) * planes + j
+
+    def send(kind, j, src, dst, to):
+        n = number(kind, j)
+        copy = pltpu.make_async_remote_copy(
+            src_ref=src, dst_ref=dst, send_sem=send_sem.at[n], recv_sem=recv_sem.at[n],
+            device_id=to, device_id_type=MESH,
+        )
+        copy.start()
+        sent.append(copy)
+
+    def arrive(kind, j, dst, to):
+        n = number(kind, j)
+        pltpu.make_async_remote_copy(
+            src_ref=dst, dst_ref=dst, send_sem=send_sem.at[n], recv_sem=recv_sem.at[n],
+            device_id=to, device_id_type=MESH,
+        ).wait_recv()
+
+    to_x, to_y, to_core = {"ep": peer_x}, {"ep": peer_y}, {"dp": 1 - core}
+    own = block(0, 0, 0)
+    mine = pl.ds(pl.multiple_of(core * half, half), half)
+    first = [
+        pltpu.make_async_copy(x_hbm.at[mine], data.at[0, own], load_sem.at[0]),
+        pltpu.make_async_copy(g_hbm.at[mine], data.at[1, own], load_sem.at[1]),
+    ]
+    loads = [
+        pltpu.make_async_copy(wg_hbm.at[0], wgv, load_sem.at[2]),
+        pltpu.make_async_copy(wu_hbm.at[0], wuv, load_sem.at[3]),
+        pltpu.make_async_copy(wd_hbm.at[0], wdv, load_sem.at[4]),
+    ]
+    for copy in first + loads:
+        copy.start()
+
+    barrier = pltpu.get_barrier_semaphore()
+    greeted = [to_x, to_y, to_core] + [{"ep": peer_z[j]} for j in range(1, planes)]
+    for other in greeted:
+        pl.semaphore_signal(barrier, inc=1, device_id=other, device_id_type=MESH)
+    pl.semaphore_wait(barrier, len(greeted))
+    for copy in first:
+        copy.wait()
+
+    def gather(j):
+        here = data.at[:, block(j, 0, 0), :]
+        if j > 0:
+            arrive("agz", j, here, {"ep": peer_z[j]})
+        send("agx", j, here, here, to_x)
+        send("agy", j, here, here, to_y)
+        if j == 0:
+            for i in range(1, planes):
+                send("agz", i, here, here, {"ep": peer_z[i]})
+
+    def forward(j):
+        from_x = block(j, 0, 1)
+        arrive("agx", j, data.at[:, from_x, :], to_x)
+        piece = data.at[:, from_x, pl.ds(0, cut)]
+        send("fa", j, piece, piece, to_y)
+        from_y = block(j, 1, 0)
+        arrive("agy", j, data.at[:, from_y, :], to_y)
+        piece = data.at[:, from_y, pl.ds(cut, cut)]
+        send("fb", j, piece, piece, to_x)
+
+    def compute(j):
+        far = block(j, 1, 1)
+        arrive("fa", j, data.at[:, far, pl.ds(0, cut)], to_y)
+        arrive("fb", j, data.at[:, far, pl.ds(cut, cut)], to_x)
+        rows = pl.ds(pl.multiple_of(zs[j] * 4 * half, 4 * half), 4 * half)
+        tile = 256
+
+        @pl.loop(0, hidden // tile)
+        def _(f):
+            cols = pl.ds(pl.multiple_of(f * tile, tile), tile)
+            tokens = data[0, rows, :]
+            gate = jnp.dot(tokens, wgv[:, cols], preferred_element_type=jnp.float32)
+            up = jnp.dot(tokens, wuv[:, cols], preferred_element_type=jnp.float32)
+            grad = lax.dot_general(data[1, rows, :], wdv[cols, :], NT, preferred_element_type=jnp.float32)
+            s = jax.nn.sigmoid(gate)
+            gg[:, cols] = (grad * up * s * (1.0 + gate * (1.0 - s))).astype(jnp.bfloat16)
+            ug[:, cols] = (grad * gate * s).astype(jnp.bfloat16)
+
+        wide = 512
+
+        @pl.loop(0, features // wide)
+        def _(d):
+            cols = pl.ds(pl.multiple_of(d * wide, wide), wide)
+            back = lax.dot_general(gg[...], wgv[cols, :], NT, preferred_element_type=jnp.float32)
+            back = back + lax.dot_general(ug[...], wuv[cols, :], NT, preferred_element_type=jnp.float32)
+            part[rows, cols] = (back * w_ref[rows, :]).astype(jnp.bfloat16)
+
+    def reduce1(j):
+        far = block(j, 1, 1)
+        send("r1a", j, part.at[far, pl.ds(0, cut)], r1a.at[j], to_y)
+        send("r1b", j, part.at[far, pl.ds(cut, cut)], r1b.at[j], to_x)
+
+    def reduce2(j):
+        side = block(j, 0, 1)
+        arrive("r1a", j, r1a.at[j], to_y)
+        part[side, 0:cut] = (part[side, 0:cut].astype(jnp.float32) + r1a[j].astype(jnp.float32)).astype(jnp.bfloat16)
+        send("r2x", j, part.at[side], r2x.at[j], to_x)
+        side = block(j, 1, 0)
+        arrive("r1b", j, r1b.at[j], to_x)
+        part[side, cut:] = (part[side, cut:].astype(jnp.float32) + r1b[j].astype(jnp.float32)).astype(jnp.bfloat16)
+        send("r2y", j, part.at[side], r2y.at[j], to_y)
+
+    def reduce3(j):
+        here = block(j, 0, 0)
+        arrive("r2x", j, r2x.at[j], to_x)
+        arrive("r2y", j, r2y.at[j], to_y)
+        if j > 0:
+            total = part[here, :].astype(jnp.float32) + r2x[j].astype(jnp.float32) + r2y[j].astype(jnp.float32)
+            part[here, :] = total.astype(jnp.bfloat16)
+            send("r3", j, part.at[here], r3.at[j], {"ep": peer_z[j]})
+
+    steps = [(gather, 0), (forward, 0), (gather, 1)]
+    for j in range(planes):
+        if j == 0:
+            for copy in loads:
+                steps.append((lambda _, c=copy: c.wait(), 0))
+        steps += [(compute, j), (reduce1, j)]
+        if j + 1 < planes:
+            steps.append((forward, j + 1))
+        if j + 2 < planes:
+            steps.append((gather, j + 2))
+        if j >= 1:
+            steps.append((reduce3, j - 1))
+        steps.append((reduce2, j))
+    steps.append((reduce3, planes - 1))
+    for step, j in steps:
+        step(j)
+
+    for j in range(1, planes):
+        arrive("r3", j, r3.at[j], {"ep": peer_z[j]})
+    for h in range(2):
+        cols = slice(h * cut, (h + 1) * cut)
+        total = part[own, cols].astype(jnp.float32)
+        total = total + r2x[0, :, cols].astype(jnp.float32) + r2y[0, :, cols].astype(jnp.float32)
+        for j in range(1, planes):
+            total = total + r3[j, :, cols].astype(jnp.float32)
+        fin[h] = total.astype(jnp.bfloat16)
+    keep = pltpu.make_async_copy(fin.at[core], out_ref.at[mine], load_sem.at[5])
+    keep.start()
+    send("dp", 0, fin.at[1 - core], out_ref.at[mine], to_core)
+    theirs = pl.ds(pl.multiple_of((1 - core) * half, half), half)
+    arrive("dp", 0, out_ref.at[theirs], to_core)
+    keep.wait()
+    for copy in sent:
+        copy.wait_send()
+
+
+def weights_of(expert_ids, gate_probs, experts, half, core):
+    ids = lax.dynamic_slice_in_dim(expert_ids, core * half, half, 0)
+    probs = lax.dynamic_slice_in_dim(gate_probs, core * half, half, 0)
+    names = jnp.arange(experts, dtype=jnp.int32)
+    table = jnp.sum(
+        jnp.where(ids[None, :, :] == names[:, None, None], probs[None, :, :], 0.0), axis=2
+    )
+    return lax.all_to_all(table, "ep", split_axis=0, concat_axis=0, tiled=True).reshape(-1)
+
+
+def fused(layer_input, out_grad, expert_ids, gate_probs, gate_proj, up_proj, down_proj):
+    experts, halves = lax.axis_size("ep"), lax.axis_size("dp")
+    tok_rows, features = layer_input.shape
+    hidden = gate_proj.shape[2]
+    half = tok_rows // halves
+    planes = experts // 4
+    weight = weights_of(expert_ids, gate_probs, experts, half, lax.axis_index("dp"))
+    rows, cut, bf16 = experts * half, features // 2, jnp.bfloat16
+    vmem, hbm = pl.BlockSpec(memory_space=pltpu.VMEM), pl.BlockSpec(memory_space=pl.ANY)
+    count = 10 * planes + 1
+    return pl.pallas_call(
+        functools.partial(kernel, planes),
+        name="fused_backward",
+        out_shape=jax.ShapeDtypeStruct((tok_rows, features // halves), bf16),
+        in_specs=[hbm, hbm, vmem, hbm, hbm, hbm],
+        out_specs=vmem,
+        scratch_shapes=[
+            pltpu.VMEM((2, rows, features), bf16),
+            pltpu.VMEM((rows, features), bf16),
+            pltpu.VMEM((features, hidden), bf16),
+            pltpu.VMEM((features, hidden), bf16),
+            pltpu.VMEM((hidden, features), bf16),
+            pltpu.VMEM((4 * half, hidden), bf16),
+            pltpu.VMEM((4 * half, hidden), bf16),
+            pltpu.VMEM((planes, half, cut), bf16),
+            pltpu.VMEM((planes, half, cut), bf16),
+            pltpu.VMEM((planes, half, features), bf16),
+            pltpu.VMEM((planes, half, features), bf16),
+            pltpu.VMEM((planes, half, features), bf16),
+            pltpu.VMEM((halves, half, cut), bf16),
+            pltpu.SemaphoreType.DMA((count,)),
+            pltpu.SemaphoreType.DMA((count,)),
+            pltpu.SemaphoreType.DMA((6,)),
+        ],
+        compiler_params=pltpu.CompilerParams(
+            collective_id=0, has_side_effects=True, vmem_limit_bytes=67043328
+        ),
+    )(layer_input, out_grad, weight[:, None], gate_proj, up_proj, down_proj)
+
+
+def dense(layer_input, out_grad, expert_ids, gate_probs, gate_proj, up_proj, down_proj):
     experts = lax.axis_size("ep")
     halves = lax.axis_size("dp")
     tok_rows, features = layer_input.shape
@@ -37,6 +272,16 @@
     return lax.all_to_all(mine, "dp", split_axis=1, concat_axis=0, tiled=True)
 
 
+def body(*args):
+    experts, halves = lax.axis_size("ep"), lax.axis_size("dp")
+    tok_rows, features = args[0].shape
+    hidden = args[4].shape[2]
+    rows = experts * tok_rows // halves
+    held = 2 * features * (3 * rows + 3 * hidden + rows)
+    fits = held < 58 * 2**20 and halves == 2 and experts % 4 == 0
+    return (fused if fits else dense)(*args)
+
+
 def solution(mesh):
     row = P("ep", None)
     mat = P("ep", None, None)

time: 443 us -> 233 us (0.53)
  waiting for transfers between devices: 338 us -> 0 us
  Pallas kernels: 0 us -> 214 us
  matrix products: 67.4 us -> 0 us
  between operations: 13.2 us -> 0.02 us
  blocking collectives: 15.3 us -> 10.6 us
    pallas_call x0 -> x1, Pallas kernels: none -> 214 us  [fused(): pl.pallas_call(functools.partial(kernel, planes), name='fused_backward',...]
    all_gather x2 -> x0, waiting for transfers between devices: 178 us -> none  [the longest x1 90.3 us: body(): in_rows = lax.all_gather(mine_in, 'ep', axis=0, tiled=True)]
    reduce_scatter x1 -> x0, waiting for transfers between devices: 160 us -> none  [body(): mine = lax.psum_scatter(back, 'ep', scatter_dimension=0, tiled=True)]
    dot_general x5 -> x0, matrix products: 67.4 us -> none  [the longest x1 17.7 us: body(): lax.dot_general(up_grad, up_mat, nt, preferred_element_type=jnp.float32)]
    all_to_all x2 -> x1, blocking collectives: 15.3 us -> 10.6 us  [weights_of(): lax.all_to_all(table, 'ep', split_axis=0, concat_axis=0, tiled=True)]
  transfers between devices with their start and end apart: 3 -> 0, of which waited for: 3 -> 0; matrix products, arithmetic and copies ran while one was open for 4% -> 0% of each run, Pallas kernels for 0% -> 0%
where the time goes in v2:
time: 233 us; the launch traced here: 231 us
  Pallas kernels  214 us (92%)
  blocking collectives  10.6 us (5%)
  local copies, waits for them, and re-layouts  5.1 us (2%)
    pallas_call x1, Pallas kernels, fused(): pl.pallas_call(functools.partial(kernel, planes), name='fused_backward',...  214 us
    all_to_all x1, blocking collectives, weights_of(): lax.all_to_all(table, 'ep', split_axis=0, concat_axis=0, tiled=True)  10.6 us

profile of v2, /device:TPU:11, one launch (start us, length us, event | category | flops | bytes accessed | tf_op | source)
XLA Modules:
  0.0 230.5 jit_solution(7633229938689487585)
XLA Ops:
  0.0 0.8 constant_dynamic-slice_fusion.1
  0.8 0.8 constant_dynamic-slice_fusion
  1.5 10.6 %all_to_all.9 = f32[16,1,64]{2,1,0:T(1,128)S(1)} all-to-all(f32[16,1,64]{2,1,0:T(1,128)S(1)} %bitcast.3), channel_id=1, replica_groups=mesh['ep'=16,'dp'=2] {'ep'}, dimensions={0} | all-to-all | bytes 8192 | tf_op jit(solution)/shard_map/all_to_all | solution.py:199
  12.2 0.5 broadcast.5
  12.7 0.7 reduce.3
  13.3 1.3 broadcast_in_dim_reshape.4.w_ref
  14.6 214.1 %fused_backward.1 = bf16[128,1792]{1,0:T(8,128)(2,1)} custom-call(bf16[128,3584]{1,0:T(8,128)(2,1)} %x_hbm.1, bf16[128,3584]{1,0:T(8,128)(2,1)} %g_hbm.1, f32[1024,1]{1,0:T(8,128)} %broadcast_in_dim_reshape.4.w_ref, bf16[1,3584,1024]{2,1,0:T(8,128)(2,1)} %wg_hbm.1, bf16[1,3584,1024]{2,1,0:T(8,128)(2,1)} %wu_hbm.1, bf16[1,1024,3584]{2,1,0:T(8,128)(2,1)} %wd_hbm.1), custom_call_target="tpu_custom_call" | custom-call | tf_op jit(solution)/shard_map/fused_backward/pallas_call | solution.py:212
  228.7 1.8 copy.19
  (1 shorter events, 0.0 us)
